TPU v7x, 512 devices: a 4x2x32 block of a 4x8x32 slice. The times are simulated.
512 devices in a mesh: parts: 2 (over y), tok: 32 (over z), hid: 8 (over x, core).
Axes of the slice: x: 4, y: 2, z: 32, core: 2. Of those that a mesh axis runs over, the one named last changes fastest.
The devices are a block of a 4x8x32 slice.
Arguments:
- tokens: bfloat16 [49152, 8192], P(('parts', 'tok'), 'hid'), parts along dimension 0, may hold values from -6 to 6
- adapter_ids: int32 [49152, 1], P(('parts', 'tok')), parts along dimension 0, may hold values from 0 to 255; in each aligned block of 768 rows (0 to 767, 768 to 1535, ...) at most 9 rows name the same one
- value_weight: bfloat16 [8192, 1024], P('hid'), may hold values from -0.0625 to 0.0625
- adapter_down: bfloat16 [256, 16, 8192], P('tok', None, 'hid'), may hold values from -0.0625 to 0.0625
- adapter_up: bfloat16 [256, 16, 1024], P('tok', None, 'hid'), may hold values from -1.5 to 1.5
Outputs:
- value_out: bfloat16 [49152, 1024], P(('parts', 'tok'), 'hid'), parts along dimension 0
There are 2 independent parts, one for each index of `parts`. A program takes and returns all parts, laid end to end along the dimension named above; an argument that names none is the same for every part. Nothing has to cross between parts.
Inputs may be any that keep to these rules, and one draw needn't show every extreme that they name: `adapter_ids`: among the 768 tokens of one index of tok, each adapter id appears at most 9 times; in some of these aligned blocks one id appears exactly 9 times.
All inputs are finite; a program needn't handle non-finite values.
Results may differ from a plain program's by a relative error of at most 0.0048.
Values may be sent and summed in bfloat16 or wider, within the bound.
No kernel may reach another device: no remote copies, remote signals or barrier semaphores. Data moves between devices by JAX's collectives and lax.ppermute only.
A program may use at most 128 MiB of HBM per device.

v0:
```python
import jax
import jax.numpy as jnp
from jax import lax
from jax.sharding import PartitionSpec as P


def split_up(array, dim, size):
    dims = array.shape
    blocks = array.reshape(*dims[:dim], size, dims[dim] // size, *dims[dim + 1 :])
    return jnp.moveaxis(blocks, dim, 0)


def sum_at_owner(array, axis, dim):
    size = lax.axis_size(axis)
    blocks = lax.all_to_all(split_up(array, dim, size), axis, 0, 0, tiled=True)
    return jnp.sum(blocks, axis=0)


def from_everyone(array, axis):
    size = lax.axis_size(axis)
    return lax.all_to_all(
        jnp.broadcast_to(array[None], (size, *array.shape)), axis, 0, 0, tiled=True
    )


def taken_together(array, axis):
    everything = from_everyone(array, axis)
    return jnp.sum(everything, axis=0)


def per_device(tokens, adapter_ids, value_weight, adapter_down, adapter_up):
    tok_rows, d_local = tokens.shape
    n_tok = lax.axis_size("tok")
    adp_dev = adapter_down.shape[0]
    low_rank = adapter_down.shape[1]
    kv_local = adapter_up.shape[2]
    adapters_all = adp_dev * n_tok
    capacity = max(2, 3 * tok_rows // adapters_all)
    token_ids = adapter_ids[:, 0]
    matches = token_ids[:, None] == token_ids[None, :]
    before = lax.broadcasted_iota(jnp.int32, (tok_rows, tok_rows), 0) > lax.broadcasted_iota(
        jnp.int32, (tok_rows, tok_rows), 1
    )
    position = jnp.sum((matches & before).astype(jnp.int32), axis=1)
    slot_index = token_ids * capacity + position
    slot_rows = (
        jnp.zeros((adapters_all * capacity, d_local), jnp.bfloat16).at[slot_index].set(tokens)
    )
    base_sums = sum_at_owner(
        lax.dot_general(
            value_weight, tokens, (((0,), (1,)), ((), ())), preferred_element_type=jnp.float32
        ),
        "hid",
        0,
    )
    weights_piece = lax.all_gather(adapter_down, "tok", axis=0, tiled=True)
    piece_count = weights_piece.shape[0]
    slot_block = slot_rows
    slot_block = slot_block.reshape(piece_count, capacity, d_local)
    partial_piece = jnp.einsum(
        "acn,arn->rac", slot_block, weights_piece, preferred_element_type=jnp.float32
    )
    partial_piece = partial_piece.reshape(low_rank, piece_count * capacity)
    low_rows = taken_together(partial_piece, "hid").astype(jnp.bfloat16)
    weights_piece = lax.all_gather(adapter_up, "tok", axis=0, tiled=True)
    piece_count = weights_piece.shape[0]
    low_block = low_rows
    low_block = low_block.reshape(low_rank, piece_count, capacity)
    expanded = jnp.einsum(
        "rac,ark->ack", low_block, weights_piece, preferred_element_type=jnp.float32
    )
    delta_slots = expanded.astype(jnp.bfloat16).reshape(piece_count * capacity, kv_local)
    delta_rows = delta_slots[slot_index]
    return (base_sums.T + delta_rows.astype(jnp.float32)).astype(jnp.bfloat16)


def solution(mesh):
    in_specs = (
        P(("parts", "tok"), "hid"),
        P(("parts", "tok"), None),
        P("hid", None),
        P("tok", None, "hid"),
        P("tok", None, "hid"),
    )
    out_specs = P(("parts", "tok"), "hid")
    return jax.shard_map(
        per_device, mesh=mesh, in_specs=in_specs, out_specs=out_specs, check_vma=False
    )
```

profile of v0, /device:TPU:34, one launch (start us, length us, event | category | flops | bytes accessed | tf_op | source)
XLA Modules:
  0.0 326.7 jit_solution(3771678501328643347)
XLA Ops:
  6.5 0.0 copy-start
  6.6 0.0 all-gather.3.cloned.1.call-start
  6.6 0.7 all-gather.3.cloned.1.call-update
  7.3 0.8 copy-done
  8.1 5.0 %fusion.6 = f32[1024,768]{1,0:T(8,128)} fusion(bf16[1024,1024]{1,0:T(8,128)(2,1)S(1)} %copy-done, bf16[768,1024]{1,0:T(8,128)(2,1)} %param.5), kind=kOutput, calls=%fused_computation.15 | convolution fusion | flops 1610612736 | bytes 6815744 | tf_op jit(solution)/shard_map/dot_general | solution.py:50
  13.1 0.0 copy-start.2
  13.1 44.9 %all-to-all-start = ((f32[8,128,768]{2,1,0:T(8,128)}), f32[8,128,768]{2,1,0:T(8,128)}, u32[]{:S(2)}, u32[]{:S(2)}) async-start(f32[8,128,768]{2,1,0:T(8,128)} %bitcast.14), calls=%async_computation | async-start | bytes 6291456 | tf_op jit(solution)/shard_map/all_to_all | solution.py:15
  58.1 0.0 all-gather.5.cloned.1.call-start
  58.1 0.8 all-gather.5.cloned.1.call-update
  58.8 0.0 copy-done.2
  58.9 0.4 convert_reduce_fusion
  59.2 9.3 %scatter_custom_fusion = bf16[2304,1024]{1,0:T(8,128)(2,1)} fusion(s32[768]{0:T(1024)S(1)} %fusion.5, bf16[768,1024]{1,0:T(8,128)(2,1)} %param.5, bf16[]{:T(256)} %constant.0.clone.1), kind=kCustom, calls=%fused_computation.4 | custom fusion | bytes 4719104 | tf_op jit(solution)/shard_map/scatter | solution.py:47
  68.6 9.5 %reshape.16 = bf16[256,9,1024]{2,1,0:T(8,128)(2,1)} reshape(bf16[2304,1024]{1,0:T(8,128)(2,1)} %scatter_custom_fusion) | data formatting | bytes 9437184 | tf_op jit(solution)/shard_map/reshape | solution.py:59
  78.1 107.0 %all-gather.3.cloned.1.call-done = bf16[256,16,1024]{2,1,0:T(8,128)(2,1)} async-done(((bf16[8,16,1024]{2,1,0:T(8,128)(2,1)}), bf16[256,16,1024]{2,1,0:T(8,128)(2,1)}) %all-gather.3.cloned.1.call-update) | async-done | bytes 8388624 | tf_op jit(solution)/shard_map/all_gather | solution.py:56
  185.0 10.5 %convolution_bitcast_fusion = f32[16,256,9]{0,2,1:T(8,128)} fusion(bf16[256,9,1024]{2,1,0:T(8,128)(2,1)} %reshape.16, bf16[256,16,1024]{2,1,0:T(8,128)(2,1)} %all-gather.3.cloned.1.call-done), kind=kOutput, calls=%fused_computation.7 | convolution fusion | flops 75497472 | bytes 13254656 | tf_op jit(solution)/shard_map/acn,arn->rac/dot_general | solution.py:60
  195.6 1.6 reshape.34
  197.2 0.3 copy.15
  197.5 0.0 all-to-all-done
  197.5 1.1 broadcast_in_dim.14
  198.6 5.0 %all-to-all-start.1 = ((f32[8,16,2304]{2,1,0:T(8,128)}), f32[8,16,2304]{2,1,0:T(8,128)S(1)}, u32[]{:S(2)}, u32[]{:S(2)}) async-start(f32[8,16,2304]{2,1,0:T(8,128)} %broadcast_in_dim.14), calls=%async_computation.1 | async-start | bytes 2359296 | tf_op jit(solution)/shard_map/all_to_all | solution.py:21
  203.6 2.8 reduce_sum.29
  206.4 1.9 copy.12
  208.4 11.1 %all-to-all-done.1 = f32[8,16,2304]{2,1,0:T(8,128)S(1)} async-done(((f32[8,16,2304]{2,1,0:T(8,128)}), f32[8,16,2304]{2,1,0:T(8,128)S(1)}, u32[]{:S(2)}, u32[]{:S(2)}) %all-to-all-start.1) | async-done | bytes 1179680 | tf_op jit(solution)/shard_map/all_to_all | solution.py:21
  219.5 0.1 reduce_sum.32
  219.5 2.2 convert_element_type.21
  221.7 91.0 %all-gather.5.cloned.1.call-done = bf16[256,16,128]{2,1,0:T(8,128)(2,1)} async-done(((bf16[8,16,128]{2,1,0:T(8,128)(2,1)}), bf16[256,16,128]{2,1,0:T(8,128)(2,1)}) %all-gather.5.cloned.1.call-update) | async-done | bytes 1048592 | tf_op jit(solution)/shard_map/all_gather | solution.py:65
  312.7 3.0 convolution_convert_fusion
  315.7 0.0 copy-start.1
  315.7 1.5 reshape.17
  317.2 1.9 gather_fusion
  319.1 0.0 copy-done.1
  319.1 0.7 fusion.4
  (3 shorter events, 0.0 us)
Async XLA Ops:
  6.5 1.6 copy-start
  6.6 178.5 %all-gather.3.cloned.1.call-start = ((), (), s32[]{:S(2)}) async-start(), calls=%async_computation.2 | async-start | bytes 8650752 | tf_op jit(solution)/shard_map/all_gather | solution.py:56
  13.1 45.7 %copy-start.2 = (s32[768,1]{0,1:T(1,128)S(1)}, s32[768,1]{0,1:T(1,128)}, u32[]{:S(2)}) copy-start(s32[768,1]{0,1:T(1,128)} %param.6) | copy-start | bytes 9220
  13.1 184.4 %all-to-all-start = ((f32[8,128,768]{2,1,0:T(8,128)}), f32[8,128,768]{2,1,0:T(8,128)}, u32[]{:S(2)}, u32[]{:S(2)}) async-start(f32[8,128,768]{2,1,0:T(8,128)} %bitcast.14), calls=%async_computation | async-start | bytes 6291456 | tf_op jit(solution)/shard_map/all_to_all | solution.py:15
  58.1 254.7 %all-gather.5.cloned.1.call-start = ((), (), s32[]{:S(2)}) async-start(), calls=%async_computation.3 | async-start | bytes 1081344 | tf_op jit(solution)/shard_map/all_gather | solution.py:65
  198.6 20.9 %all-to-all-start.1 = ((f32[8,16,2304]{2,1,0:T(8,128)}), f32[8,16,2304]{2,1,0:T(8,128)S(1)}, u32[]{:S(2)}, u32[]{:S(2)}) async-start(f32[8,16,2304]{2,1,0:T(8,128)} %broadcast_in_dim.14), calls=%async_computation.1 | async-start | bytes 2359296 | tf_op jit(solution)/shard_map/all_to_all | solution.py:21
  315.7 3.4 %copy-start.1 = (f32[128,768]{0,1:T(8,128)S(1)}, f32[128,768]{0,1:T(8,128)}, u32[]{:S(2)}) copy-start(f32[128,768]{0,1:T(8,128)} %copy.12) | copy-start | bytes 1179652
Sparse Core Ops, SparseCore 0:
  9.4 175.5 all-gather.2
  187.1 125.5 all-gather.4
where the time goes:
time: 327 us
  waiting for transfers between devices  211 us (65%)
  starting transfers between devices  49.9 us (15%)
  local copies, waits for them, and re-layouts  30.2 us (9%)
  matrix products  18.6 us (6%)
  between operations  13.5 us (4%)
  other arithmetic  4.02 us (1%)
    all_gather x1, waiting for transfers between devices, per_device(): weights_piece = lax.all_gather(adapter_down, 'tok', axis=0, tiled=True)  107 us
    all_gather x1, waiting for transfers between devices, per_device(): weights_piece = lax.all_gather(adapter_up, 'tok', axis=0, tiled=True)  91 us
    all_to_all x1, starting transfers between devices, sum_at_owner(): blocks = lax.all_to_all(split_up(array, dim, size), axis, 0, 0, tiled=True)  44.9 us
    all_to_all x1, waiting for transfers between devices, from_everyone(): lax.all_to_all(jnp.broadcast_to(array[None], (size, *array.shape)), axis,...  11.1 us
    dot_general x1, matrix products, per_device(): jnp.einsum('acn,arn->rac', slot_block, weights_piece, preferred_element_t...  10.5 us
    reshape x1, local copies, waits for them, and re-layouts, per_device(): slot_block = slot_block.reshape(piece_count, capacity, d_local)  9.49 us
    scatter x1, local copies, waits for them, and re-layouts, per_device(): jnp.zeros((adapters_all * capacity, d_local), jnp.bfloat16).at[slot_index]  9.33 us
  transfers between devices with their start and end apart: 4, of which 3 were waited for; matrix products, arithmetic and copies ran while one was open for 14% of the time, Pallas kernels for 0%

commit v1 on v0

--- a/solution.py
+++ b/solution.py
@@ -53,7 +53,11 @@
         "hid",
         0,
     )
-    weights_piece = lax.all_gather(adapter_down, "tok", axis=0, tiled=True)
+    peers = lax.axis_size("tok")
+    repeats = [peers if d == 0 else 1 for d in range(adapter_down.ndim)]
+    weights_piece = lax.all_to_all(
+        jnp.tile(adapter_down, repeats), "tok", split_axis=0, concat_axis=0, tiled=True
+    )
     piece_count = weights_piece.shape[0]
     slot_block = slot_rows
     slot_block = slot_block.reshape(piece_count, capacity, d_local)

time: 327 us -> 938 us (2.87)
  waiting for transfers between devices: 211 us -> 810 us
    all_to_all x0 -> x1, waiting for transfers between devices: none -> 707 us  [per_device(): lax.all_to_all(jnp.tile(adapter_down, repeats), 'tok', split_axis=0, conc...]
    all_gather x1 -> x0, waiting for transfers between devices: 107 us -> none  [per_device(): weights_piece = lax.all_gather(adapter_down, 'tok', axis=0, tiled=True)]
    all_to_all x0 -> x1, starting transfers between devices: none -> 45.8 us  [per_device(): lax.all_to_all(jnp.tile(adapter_down, repeats), 'tok', split_axis=0, conc...]
    all_to_all x1, starting transfers between devices: 44.9 us -> 5.11 us  [sum_at_owner(): blocks = lax.all_to_all(split_up(array, dim, size), axis, 0, 0, tiled=True)]
  transfers between devices with their start and end apart: 4 -> 4, of which waited for: 3 -> 4; matrix products, arithmetic and copies ran while one was open for 14% -> 5% of each run, Pallas kernels for 0% -> 0%
where the time goes in v1:
time: 938 us; the launch traced here: 937 us
  waiting for transfers between devices  810 us (86%)
  starting transfers between devices  55.9 us (6%)
  local copies, waits for them, and re-layouts  34.7 us (4%)
  matrix products  18.6 us (2%)
  between operations  13.5 us (1%)
    all_to_all x1, waiting for transfers between devices, per_device(): lax.all_to_all(jnp.tile(adapter_down, repeats), 'tok', split_axis=0, conc...  707 us
    all_gather x1, waiting for transfers between devices, per_device(): weights_piece = lax.all_gather(adapter_up, 'tok', axis=0, tiled=True)  86.7 us
    all_to_all x1, starting transfers between devices, per_device(): lax.all_to_all(jnp.tile(adapter_down, repeats), 'tok', split_axis=0, conc...  45.8 us
  transfers between devices with their start and end apart: 4, of which 4 were waited for; matrix products, arithmetic and copies ran while one was open for 5% of the time, Pallas kernels for 0%

profile of v1, /device:TPU:34, one launch (start us, length us, event | category | flops | bytes accessed | tf_op | source)
XLA Modules:
  0.0 936.8 jit_solution(4342281210261695634)
XLA Ops:
  6.5 0.0 copy-start
  6.6 5.4 tile.4
  11.9 45.8 %all-to-all-start.1 = ((bf16[256,16,1024]{2,1,0:T(8,128)(2,1)}), bf16[256,16,1024]{2,1,0:T(8,128)(2,1)}, u32[]{:S(2)}, u32[]{:S(2)}) async-start(bf16[256,16,1024]{2,1,0:T(8,128)(2,1)} %bitcast.15), calls=%async_computation.1 | async-start | bytes 16777216 | tf_op jit(solution)/shard_map/all_to_all | solution.py:58
  57.7 0.0 copy-done
  57.7 5.0 fusion.6
  62.7 706.9 %all-to-all-done.1 = bf16[256,16,1024]{2,1,0:T(8,128)(2,1)} async-done(((bf16[256,16,1024]{2,1,0:T(8,128)(2,1)}), bf16[256,16,1024]{2,1,0:T(8,128)(2,1)}, u32[]{:S(2)}, u32[]{:S(2)}) %all-to-all-start.1) | async-done | bytes 8388640 | tf_op jit(solution)/shard_map/all_to_all | solution.py:58
  769.6 0.0 copy-start.2
  769.6 5.1 all-to-all-start
  774.7 0.0 all-gather.2.cloned.1.call-start
  774.7 0.7 all-gather.2.cloned.1.call-update
  775.5 0.0 copy-done.2
  775.5 0.4 convert_reduce_fusion
  775.9 9.3 scatter_custom_fusion
  785.2 9.5 %reshape.20 = bf16[256,9,1024]{2,1,0:T(8,128)(2,1)} reshape(bf16[2304,1024]{1,0:T(8,128)(2,1)} %scatter_custom_fusion) | data formatting | bytes 9437184 | tf_op jit(solution)/shard_map/reshape | solution.py:63
  794.7 10.5 %convolution_bitcast_fusion = f32[16,256,9]{0,2,1:T(8,128)} fusion(bf16[256,9,1024]{2,1,0:T(8,128)(2,1)} %reshape.20, bf16[256,16,1024]{2,1,0:T(8,128)(2,1)} %all-to-all-done.1), kind=kOutput, calls=%fused_computation.7 | convolution fusion | flops 75497472 | bytes 13254656 | tf_op jit(solution)/shard_map/acn,arn->rac/dot_general | solution.py:64
  805.2 1.6 reshape.38
  806.8 0.3 copy.15
  807.1 4.6 all-to-all-done
  811.8 1.1 broadcast_in_dim.14
  812.8 5.0 all-to-all-start.2
  817.8 2.8 reduce_sum.29
  820.7 1.9 copy.12
  822.6 11.2 %all-to-all-done.2 = f32[8,16,2304]{2,1,0:T(8,128)S(1)} async-done(((f32[8,16,2304]{2,1,0:T(8,128)}), f32[8,16,2304]{2,1,0:T(8,128)S(1)}, u32[]{:S(2)}, u32[]{:S(2)}) %all-to-all-start.2) | async-done | bytes 1179680 | tf_op jit(solution)/shard_map/all_to_all | solution.py:21
  833.8 0.1 reduce_sum.32
  833.8 2.2 convert_element_type.21
  836.1 86.7 %all-gather.2.cloned.1.call-done = bf16[256,16,128]{2,1,0:T(8,128)(2,1)} async-done(((bf16[8,16,128]{2,1,0:T(8,128)(2,1)}), bf16[256,16,128]{2,1,0:T(8,128)(2,1)}) %all-gather.2.cloned.1.call-update) | async-done | bytes 1048592 | tf_op jit(solution)/shard_map/all_gather | solution.py:69
  922.8 3.0 convolution_convert_fusion
  925.8 0.0 copy-start.1
  925.8 1.5 reshape.21
  927.3 1.9 gather_fusion
  929.2 0.0 copy-done.1
  929.2 0.7 fusion.4
  (3 shorter events, 0.0 us)
Async XLA Ops:
  6.5 51.2 %copy-start = (bf16[1024,1024]{1,0:T(8,128)(2,1)S(1)}, bf16[1024,1024]{1,0:T(8,128)(2,1)}, u32[]{:S(2)}) copy-start(bf16[1024,1024]{1,0:T(8,128)(2,1)} %param.7) | copy-start | bytes 6291460
  11.9 757.7 %all-to-all-start.1 = ((bf16[256,16,1024]{2,1,0:T(8,128)(2,1)}), bf16[256,16,1024]{2,1,0:T(8,128)(2,1)}, u32[]{:S(2)}, u32[]{:S(2)}) async-start(bf16[256,16,1024]{2,1,0:T(8,128)(2,1)} %bitcast.15), calls=%async_computation.1 | async-start | bytes 16777216 | tf_op jit(solution)/shard_map/all_to_all | solution.py:58
  769.6 5.9 copy-start.2
  769.6 42.2 %all-to-all-start = ((f32[8,128,768]{2,1,0:T(8,128)}), f32[8,128,768]{2,1,0:T(8,128)}, u32[]{:S(2)}, u32[]{:S(2)}) async-start(f32[8,128,768]{2,1,0:T(8,128)} %bitcast.16), calls=%async_computation | async-start | bytes 6291456 | tf_op jit(solution)/shard_map/all_to_all | solution.py:15
  774.7 148.1 %all-gather.2.cloned.1.call-start = ((), (), s32[]{:S(2)}) async-start(), calls=%async_computation.3 | async-start | bytes 1081344 | tf_op jit(solution)/shard_map/all_gather | solution.py:69
  812.8 20.9 %all-to-all-start.2 = ((f32[8,16,2304]{2,1,0:T(8,128)}), f32[8,16,2304]{2,1,0:T(8,128)S(1)}, u32[]{:S(2)}, u32[]{:S(2)}) async-start(f32[8,16,2304]{2,1,0:T(8,128)} %broadcast_in_dim.14), calls=%async_computation.2 | async-start | bytes 2359296 | tf_op jit(solution)/shard_map/all_to_all | solution.py:21
  925.8 3.4 copy-start.1
Sparse Core Ops, SparseCore 0:
  777.6 145.1 all-gather.1
